TPU v7x, 32 devices: a whole 2x2x4 slice. The times are simulated.
32 devices in a mesh: dof: 16 (over z, x, core), mode: 2 (over y).
Axes of the slice: x: 2, y: 2, z: 4, core: 2. Of those that a mesh axis runs over, the one named last changes fastest.
Arguments:
- stiffness_tiles: bfloat16 [512, 10, 128, 128], P('dof'), may hold values from -0.15625 to 0.15625
- tile_cols: int32 [512, 10], P('dof'), may hold values from 0 to 47, as said below
- send_rows: int32 [32, 8], P('dof'), may hold values from 0 to 31, as said below
- block: bfloat16 [65536, 128], P('dof', 'mode'), may hold values from -51 to 51
- lower_bound: float32 [1], replicated, may hold values from -1.2 to -0.6
- upper_bound: float32 [1], replicated, may hold values from 0.4 to 0.9
Outputs:
- basis: bfloat16 [65536, 128], P('dof', 'mode')
- ritz: float32 [128, 128], replicated
Inputs may be any that keep to these rules, and one draw needn't show every extreme that they name: `tile_cols`: entry 0 of every tile row is that row's own local index; entry 1 is a code of the lower neighbour's upward list and entry 2 a code of the upper neighbour's downward list. A code below 32 is a tile row of the same partition; 32 + s is slot s of the lower neighbour's upward list; 40 + s is slot s of the upper neighbour's downward list. `send_rows`: rows 2 p and 2 p + 1 hold distinct local tile rows of partition p: its downward and upward send lists.
All inputs are finite; a program needn't handle non-finite values.
Results may differ from a plain program's by a relative error of at most 0.0086.
Values may be sent and summed in bfloat16 or wider, within the bound.
A program may use at most 64 MiB of HBM per device.

v0:
```python
import functools

import jax
import jax.numpy as jnp
from jax import lax
from jax.experimental import pallas as pl
from jax.experimental.pallas import tpu as pltpu
from jax.sharding import PartitionSpec as P

MESH = pl.DeviceIdType.MESH
NT = (((1,), (1,)), ((), ()))
NN = (((1,), (0,)), ((), ()))
TN = (((0,), (0,)), ((), ()))
EXACT = lax.Precision.HIGHEST


def kernel(
    parts, cols, rows, low_ref, high_ref, x_ref, a_hbm, basis_ref, ritz_ref,
    a_ref, level0, level1, level2, plain, image, other, sends, ar_send, ar_recv,
    whole, final_send, final_recv, work, inv_ref, inv_t,
    a_sem, halo_send, halo_recv, mode_send, mode_recv, ar_ssem, ar_rsem,
):
    tiles, nnz, size = a_ref.shape[0], a_ref.shape[1], a_ref.shape[2]
    modes = x_ref.shape[0]
    width = 2 * modes
    slots = rows.shape[1]
    stages = ar_send.shape[0] - 1
    chunks = mode_send.shape[0]
    part_rows = tiles // chunks
    p = lax.axis_index("dof")
    my = lax.axis_index("mode")
    has_low = p > 0
    has_up = p < parts - 1

    loads = []
    a_parts = a_sem.shape[0]
    for i in range(a_parts):
        span = pl.ds(i * (tiles // a_parts), tiles // a_parts)
        loads.append(pltpu.make_async_copy(a_hbm.at[span], a_ref.at[span], a_sem.at[i]))
        loads[-1].start()

    def flipped(bit):
        return p + bit * (1 - 2 * ((p // bit) % 2))

    barrier = pltpu.get_barrier_semaphore()
    for s in range(stages):
        pl.semaphore_signal(barrier, inc=1, device_id=(flipped(1 << s), my), device_id_type=MESH)
    pl.semaphore_signal(barrier, inc=1, device_id=(p, 1 - my), device_id_type=MESH)

    @pl.when(has_low)
    def _():
        pl.semaphore_signal(barrier, inc=1, device_id=(p - 1, my), device_id_type=MESH)

    @pl.when(has_up)
    def _():
        pl.semaphore_signal(barrier, inc=1, device_id=(p + 1, my), device_id_type=MESH)

    for t in range(tiles):
        tile = x_ref[:, t * size : (t + 1) * size]
        level0[t] = tile
        plain[t] = tile

    @pl.when(p == 0)
    def _():
        for level in (level0, level1, level2):
            level[tiles : tiles + slots] = jnp.zeros((slots, modes, size), jnp.bfloat16)

    @pl.when(p == parts - 1)
    def _():
        for level in (level0, level1, level2):
            level[tiles + slots :] = jnp.zeros((slots, modes, size), jnp.bfloat16)

    for s in range(slots):
        sends[0, s] = plain[rows[1, s]]
        sends[0, slots + s] = plain[rows[0, s]]

    pl.semaphore_wait(
        barrier, stages + 1 + has_low.astype(jnp.int32) + has_up.astype(jnp.int32)
    )

    def halo(index, level):
        up = pltpu.make_async_remote_copy(
            src_ref=sends.at[index, pl.ds(0, slots)],
            dst_ref=level.at[pl.ds(tiles, slots)],
            send_sem=halo_send.at[index, 0],
            recv_sem=halo_recv.at[index, 0],
            device_id=(lax.rem(p + 1, parts), my),
            device_id_type=MESH,
        )
        down = pltpu.make_async_remote_copy(
            src_ref=sends.at[index, pl.ds(slots, slots)],
            dst_ref=level.at[pl.ds(tiles + slots, slots)],
            send_sem=halo_send.at[index, 1],
            recv_sem=halo_recv.at[index, 1],
            device_id=(lax.rem(p + parts - 1, parts), my),
            device_id_type=MESH,
        )
        return up, down

    def start_halo(index, level):
        up, down = halo(index, level)
        pl.when(has_up)(up.start)
        pl.when(has_low)(down.start)

    def wait_halo(index, level):
        up, down = halo(index, level)
        pl.when(has_low)(up.wait_recv)
        pl.when(has_up)(down.wait_recv)
        pl.when(has_up)(up.wait_send)
        pl.when(has_low)(down.wait_send)

    start_halo(0, level0)

    center = (high_ref[0] + low_ref[0]) * 0.5
    half_width = (high_ref[0] - low_ref[0]) * 0.5
    scale = jnp.ones((1, size), jnp.float32) / jnp.full((1, size), half_width, jnp.float32)

    def product(level, t):
        field = jnp.concatenate([level[cols[k, t]] for k in range(nnz)], axis=1)
        stored = jnp.concatenate([a_ref[t, k] for k in range(nnz)], axis=1)
        return lax.dot_general(field, stored, NT, preferred_element_type=jnp.float32)

    def first(t):
        own = level0[t].astype(jnp.float32)
        return ((product(level0, t) - center * own) * scale).astype(jnp.bfloat16)

    def second(t):
        own = level1[t].astype(jnp.float32)
        before = level0[t].astype(jnp.float32)
        return (2.0 * (product(level1, t) - center * own) * scale - before).astype(jnp.bfloat16)

    def send_tiles(index, make):
        @pl.loop(0, slots // 2)
        def _(i):
            made = []
            for u in range(2):
                s = i * 2 + u
                made.append((s, make(rows[1, s])))
                made.append((slots + s, make(rows[0, s])))
            for s, value in made:
                sends[index, s] = value

    def all_tiles(make, target, begin, count, group=4):
        @pl.loop(0, count // group)
        def _(i):
            made = [make(begin + i * group + u) for u in range(group)]
            for u in range(group):
                target[begin + i * group + u] = made[u]

    for load in loads:
        load.wait()
    wait_halo(0, level0)
    send_tiles(1, first)
    start_halo(1, level1)
    all_tiles(first, level1, 0, tiles)
    wait_halo(1, level1)
    send_tiles(2, second)
    start_halo(2, level2)

    def exchange(c):
        span = pl.ds(c * part_rows, part_rows)
        return pltpu.make_async_remote_copy(
            src_ref=level2.at[span],
            dst_ref=other.at[span],
            send_sem=mode_send.at[c],
            recv_sem=mode_recv.at[c],
            device_id=(p, 1 - my),
            device_id_type=MESH,
        )

    for c in range(chunks):
        all_tiles(second, level2, c * part_rows, part_rows)
        exchange(c).start()
    wait_halo(2, level2)
    all_tiles(lambda t: product(level2, t).astype(jnp.bfloat16), image, 0, tiles)

    total = jnp.zeros((width, width), jnp.float32)
    for c in range(chunks):
        exchange(c).wait_recv()

        def accumulate(i, acc):
            left, right = [], []
            for u in range(4):
                t = c * part_rows + i * 4 + u
                left.append(jnp.concatenate([level2[t], image[t]], axis=0))
                right.append(jnp.concatenate([level2[t], other[t]], axis=0))
            return acc + lax.dot_general(
                jnp.concatenate(left, axis=1), jnp.concatenate(right, axis=1), NT,
                preferred_element_type=jnp.float32,
            )

        total = lax.fori_loop(0, part_rows // 4, accumulate, total)
    total = jnp.where(my == 1, pltpu.roll(total, modes, 1), total)

    core = lax.rem(p, 2)
    start_own = pl.multiple_of(core * modes, modes)
    start_out = pl.multiple_of((1 - core) * modes, modes)
    whole[...] = total

    def transfer(s, source, target, partner):
        copy = pltpu.make_async_remote_copy(
            src_ref=source,
            dst_ref=target,
            send_sem=ar_ssem.at[s],
            recv_sem=ar_rsem.at[s],
            device_id=partner,
            device_id_type=MESH,
        )
        copy.start()
        copy.wait()

    transfer(0, whole.at[pl.ds(start_out, modes)], ar_recv.at[0], (flipped(1), my))
    part = whole[pl.ds(start_own, modes), :] + ar_recv[0]
    for s in range(1, stages + 1):
        partner = (flipped(1 << s), my) if s < stages else (p, 1 - my)
        ar_send[s] = part
        transfer(s, ar_send.at[s], ar_recv.at[s], partner)
        if s < stages:
            part = part + ar_recv[s]
    theirs = ar_recv[stages]
    low_part = jnp.where(my == 0, part, theirs)
    high_part = jnp.where(my == 0, theirs, part)
    final_send[:modes] = low_part
    final_send[modes:] = high_part
    transfer(stages + 1, final_send, final_recv, (flipped(1), my))
    mine, received = final_send[...], final_recv[...]
    count = parts * tiles * size
    gram = jnp.where(core == 0, mine, received) / count
    projected_t = jnp.where(core == 0, received, mine) / count

    step = 16
    row_id = lax.broadcasted_iota(jnp.int32, (width, width), 0)
    col_id = lax.broadcasted_iota(jnp.int32, (width, width), 1)
    work[:, :width] = gram
    work[:, width:] = (row_id == col_id).astype(jnp.float32)
    small = lax.broadcasted_iota(jnp.int32, (step, 1), 0)
    lanes = lax.broadcasted_iota(jnp.int32, (step, width), 1)

    @pl.loop(0, width // step)
    def _(b):
        begin = pl.multiple_of(b * step, step)
        panel = work[pl.ds(begin, step), :]
        near = panel[:, :width]
        columns = [
            jnp.sum(jnp.where(lanes == begin + s, near, 0.0), axis=1, keepdims=True)
            for s in range(step)
        ]
        pivots = jnp.zeros((step, 1), jnp.float32)
        for q in range(step):
            pivot = columns[q][q : q + 1, :]
            pivots = jnp.where(small == q, pivot, pivots)
            if q == step - 1:
                break
            factor = jnp.where(small > q, columns[q] / pivot, 0.0)
            panel = panel - factor * panel[q : q + 1, :]
            for s in range(q + 1, step):
                columns[s] = columns[s] - factor * columns[s][q : q + 1, :]
        inv_ref[pl.ds(begin, step), :] = panel[:, width:] / jnp.sqrt(pivots)
        below = jnp.where(lanes >= begin + step, panel[:, :width] / pivots, 0.0)
        work[...] = work[...] - lax.dot_general(
            below, panel, TN, precision=EXACT, preferred_element_type=jnp.float32
        )

    inverse = inv_ref[...]
    half = lax.dot_general(
        inverse, projected_t, NT, precision=EXACT, preferred_element_type=jnp.float32
    )
    ritz_ref[...] = lax.dot_general(
        half, inverse, NT, precision=EXACT, preferred_element_type=jnp.float32
    )
    own = jnp.where(my == 0, inverse[:modes], pltpu.roll(inverse[modes:], modes, 1))
    inv_t[...] = own.astype(jnp.bfloat16)
    for t in range(0, tiles, 2):
        pair = jnp.concatenate(
            [jnp.concatenate([level2[u], other[u]], axis=0) for u in (t, t + 1)], axis=1
        )
        basis_ref[:, t * size : (t + 2) * size] = lax.dot_general(
            inv_t[...], pair, NN, preferred_element_type=jnp.float32
        ).astype(jnp.bfloat16)
    for c in range(chunks):
        exchange(c).wait_send()


def shards(parts, stiffness_tiles, tile_cols, send_rows, block, lower_bound, upper_bound):
    row_count, modes = block.shape
    tiles, nnz, size = stiffness_tiles.shape[:3]
    slots = send_rows.shape[1]
    width = 2 * modes
    stages = parts.bit_length() - 1
    assert 1 << stages == parts
    chunks = 4
    smem = pl.BlockSpec(memory_space=pltpu.SMEM)
    vmem = pl.BlockSpec(memory_space=pltpu.VMEM)
    dma = pltpu.SemaphoreType.DMA
    level = pltpu.VMEM((tiles + 2 * slots, modes, size), jnp.bfloat16)
    field = pltpu.VMEM((tiles, modes, size), jnp.bfloat16)
    basis, ritz = pl.pallas_call(
        functools.partial(kernel, parts),
        out_shape=(
            jax.ShapeDtypeStruct((modes, row_count), jnp.bfloat16),
            jax.ShapeDtypeStruct((width, width), jnp.float32),
        ),
        in_specs=[smem, smem, smem, smem, vmem, pl.BlockSpec(memory_space=pl.ANY)],
        out_specs=(vmem, vmem),
        scratch_shapes=[
            pltpu.VMEM(stiffness_tiles.shape, jnp.bfloat16),
            level, level, level, field, field, field,
            pltpu.VMEM((3, 2 * slots, modes, size), jnp.bfloat16),
            pltpu.VMEM((stages + 1, modes, width), jnp.float32),
            pltpu.VMEM((stages + 1, modes, width), jnp.float32),
            pltpu.VMEM((width, width), jnp.float32),
            pltpu.VMEM((width, width), jnp.float32),
            pltpu.VMEM((width, width), jnp.float32),
            pltpu.VMEM((width, 2 * width), jnp.float32),
            pltpu.VMEM((width, width), jnp.float32),
            pltpu.VMEM((modes, width), jnp.bfloat16),
            dma((4,)), dma((3, 2)), dma((3, 2)), dma((chunks,)), dma((chunks,)),
            dma((stages + 2,)), dma((stages + 2,)),
        ],
        compiler_params=pltpu.CompilerParams(
            collective_id=0, has_side_effects=True, vmem_limit_bytes=60 * 1024 * 1024
        ),
    )(tile_cols.T, send_rows, lower_bound, upper_bound, block.T, stiffness_tiles)
    return basis.T, ritz


def solution(mesh):
    placed = (
        P("dof", None, None, None),
        P("dof", None),
        P("dof", None),
        P("dof", "mode"),
        P(),
        P(),
    )
    return jax.shard_map(
        functools.partial(shards, mesh.shape["dof"]),
        mesh=mesh, in_specs=placed, out_specs=(P("dof", "mode"), P()), check_vma=False,
    )
```

profile of v0, /device:TPU:0, one launch (start us, length us, event | category | flops | bytes accessed | tf_op | source)
XLA Modules:
  0.0 58.5 jit_solution(14102258932626489051)
XLA Ops:
  1.9 53.2 %shard_map.77 = (bf16[64,4096]{1,0:T(8,128)(2,1)}, f32[128,128]{1,0:T(8,128)}) custom-call(s32[10,32]{1,0:T(8,128)} %bitcast.5, s32[2,8]{1,0:T(2,128)} %rows.1, f32[1]{0:T(128)S(6)} %copy.10.low_ref, f32[1]{0:T(128)S(6)} %copy.11.high_ref, bf16[64,4096]{1,0:T(8,128)(2,1)} %bitcast.4, bf16[32,10,128,128]{3,2,1,0:T(8,128)(2,1)} %a_hbm.1), custom_call_target="tpu_custom_call" | custom-call | tf_op jit(solution)/shard_map/pallas_call | solution.py:297
  55.2 1.9 %copy.12 = bf16[4096,64]{0,1:T(8,128)(2,1)} copy(bf16[4096,64]{0,1:T(8,128)(2,1)} %bitcast.3) | data formatting | bytes 1048576
  57.0 1.5 %copy.13 = f32[128,128]{1,0:T(8,128)} copy(f32[128,128]{1,0:T(8,128)} %get-tuple-element.9) | data formatting | bytes 131072
where the time goes:
time: 58.9 us; the launch traced here: 58.5 us
  Pallas kernels  53.2 us (90%)
  local copies, waits for them, and re-layouts  3.34 us (6%)
  between operations  1.93 us (3%)
    pallas_call x1, Pallas kernels, shards(): pl.pallas_call(functools.partial(kernel, parts), out_shape=(jax.ShapeDtyp...  53.2 us
    unnamed x2, local copies, waits for them, and re-layouts  3.34 us

commit v1 on v0

--- a/solution.py
+++ b/solution.py
@@ -8,6 +8,7 @@
 from jax.sharding import PartitionSpec as P
 
 MESH = pl.DeviceIdType.MESH
+GROUP = 16
 NT = (((1,), (1,)), ((), ()))
 NN = (((1,), (0,)), ((), ()))
 TN = (((0,), (0,)), ((), ()))
@@ -15,13 +16,13 @@
 
 
 def kernel(
-    parts, cols, rows, low_ref, high_ref, x_ref, a_hbm, basis_ref, ritz_ref,
-    a_ref, level0, level1, level2, plain, image, other, sends, ar_send, ar_recv,
+    parts, cols, rows, low_ref, high_ref, x_hbm, a_hbm, basis_ref, ritz_ref,
+    a_ref, turned, level0, level1, level2, x_ref, plain, image, other, sends, ar_send, ar_recv,
     whole, final_send, final_recv, work, inv_ref, inv_t,
-    a_sem, halo_send, halo_recv, mode_send, mode_recv, ar_ssem, ar_rsem,
+    x_sem, a_sem, halo_send, halo_recv, mode_send, mode_recv, ar_ssem, ar_rsem,
 ):
     tiles, nnz, size = a_ref.shape[0], a_ref.shape[1], a_ref.shape[2]
-    modes = x_ref.shape[0]
+    modes = x_hbm.shape[0]
     width = 2 * modes
     slots = rows.shape[1]
     stages = ar_send.shape[0] - 1
@@ -32,12 +33,11 @@
     has_low = p > 0
     has_up = p < parts - 1
 
-    loads = []
-    a_parts = a_sem.shape[0]
-    for i in range(a_parts):
-        span = pl.ds(i * (tiles // a_parts), tiles // a_parts)
-        loads.append(pltpu.make_async_copy(a_hbm.at[span], a_ref.at[span], a_sem.at[i]))
-        loads[-1].start()
+    odd = lax.rem(p, 2)
+    mate = p + 1 - 2 * odd
+    far = p - 1 + 2 * odd
+    has_far = (far >= 0) & (far < parts)
+    far_slot = lax.rem(far + parts, parts)
 
     def flipped(bit):
         return p + bit * (1 - 2 * ((p // bit) % 2))
@@ -47,18 +47,26 @@
         pl.semaphore_signal(barrier, inc=1, device_id=(flipped(1 << s), my), device_id_type=MESH)
     pl.semaphore_signal(barrier, inc=1, device_id=(p, 1 - my), device_id_type=MESH)
 
-    @pl.when(has_low)
+    @pl.when(has_far)
     def _():
-        pl.semaphore_signal(barrier, inc=1, device_id=(p - 1, my), device_id_type=MESH)
-
-    @pl.when(has_up)
-    def _():
-        pl.semaphore_signal(barrier, inc=1, device_id=(p + 1, my), device_id_type=MESH)
+        pl.semaphore_signal(barrier, inc=1, device_id=(far_slot, my), device_id_type=MESH)
+
+    fetch = pltpu.make_async_copy(x_hbm, x_ref, x_sem.at[0])
+    fetch.start()
+    fetch.wait()
+    loads = []
+    a_parts = a_sem.shape[0]
+    share = tiles // a_parts
+    for i in range(a_parts):
+        span = pl.ds(i * share, share)
+        loads.append(pltpu.make_async_copy(a_hbm.at[span], a_ref.at[span], a_sem.at[i]))
+        loads[-1].start()
 
     for t in range(tiles):
-        tile = x_ref[:, t * size : (t + 1) * size]
-        level0[t] = tile
-        plain[t] = tile
+        plain[t] = x_ref[:, t * size : (t + 1) * size]
+    for s in range(slots):
+        for which, row in enumerate((rows[odd, s], rows[1 - odd, s])):
+            sends[0, which, s] = plain[row]
 
     @pl.when(p == 0)
     def _():
@@ -70,46 +78,36 @@
         for level in (level0, level1, level2):
             level[tiles + slots :] = jnp.zeros((slots, modes, size), jnp.bfloat16)
 
-    for s in range(slots):
-        sends[0, s] = plain[rows[1, s]]
-        sends[0, slots + s] = plain[rows[0, s]]
-
-    pl.semaphore_wait(
-        barrier, stages + 1 + has_low.astype(jnp.int32) + has_up.astype(jnp.int32)
-    )
-
-    def halo(index, level):
-        up = pltpu.make_async_remote_copy(
-            src_ref=sends.at[index, pl.ds(0, slots)],
-            dst_ref=level.at[pl.ds(tiles, slots)],
-            send_sem=halo_send.at[index, 0],
-            recv_sem=halo_recv.at[index, 0],
-            device_id=(lax.rem(p + 1, parts), my),
+    pl.semaphore_wait(barrier, stages + 1 + has_far.astype(jnp.int32))
+
+    def halo(index, level, remote):
+        hop = odd if remote else 1 - odd
+        return pltpu.make_async_remote_copy(
+            src_ref=sends.at[index, 0 if remote else 1],
+            dst_ref=level.at[pl.ds(tiles + slots * (1 - hop), slots)],
+            send_sem=halo_send.at[index, 0 if remote else 1],
+            recv_sem=halo_recv.at[index, 0 if remote else 1],
+            device_id=(far_slot if remote else mate, my),
             device_id_type=MESH,
         )
-        down = pltpu.make_async_remote_copy(
-            src_ref=sends.at[index, pl.ds(slots, slots)],
-            dst_ref=level.at[pl.ds(tiles + slots, slots)],
-            send_sem=halo_send.at[index, 1],
-            recv_sem=halo_recv.at[index, 1],
-            device_id=(lax.rem(p + parts - 1, parts), my),
-            device_id_type=MESH,
-        )
-        return up, down
-
-    def start_halo(index, level):
-        up, down = halo(index, level)
-        pl.when(has_up)(up.start)
-        pl.when(has_low)(down.start)
+
+    def start_far(index, level):
+        pl.when(has_far)(halo(index, level, True).start)
+
+    def start_near(index, level):
+        halo(index, level, False).start()
 
     def wait_halo(index, level):
-        up, down = halo(index, level)
-        pl.when(has_low)(up.wait_recv)
-        pl.when(has_up)(down.wait_recv)
-        pl.when(has_up)(up.wait_send)
-        pl.when(has_low)(down.wait_send)
-
-    start_halo(0, level0)
+        near, remote = halo(index, level, False), halo(index, level, True)
+        near.wait_recv()
+        near.wait_send()
+        pl.when(has_far)(remote.wait_recv)
+        pl.when(has_far)(remote.wait_send)
+
+    start_far(0, level0)
+    start_near(0, level0)
+    for t in range(tiles):
+        level0[t] = plain[t]
 
     center = (high_ref[0] + low_ref[0]) * 0.5
     half_width = (high_ref[0] - low_ref[0]) * 0.5
@@ -117,8 +115,7 @@
 
     def product(level, t):
         field = jnp.concatenate([level[cols[k, t]] for k in range(nnz)], axis=1)
-        stored = jnp.concatenate([a_ref[t, k] for k in range(nnz)], axis=1)
-        return lax.dot_general(field, stored, NT, preferred_element_type=jnp.float32)
+        return lax.dot_general(field, turned[t], NN, preferred_element_type=jnp.float32)
 
     def first(t):
         own = level0[t].astype(jnp.float32)
@@ -129,33 +126,41 @@
         before = level0[t].astype(jnp.float32)
         return (2.0 * (product(level1, t) - center * own) * scale - before).astype(jnp.bfloat16)
 
-    def send_tiles(index, make):
-        @pl.loop(0, slots // 2)
-        def _(i):
-            made = []
-            for u in range(2):
-                s = i * 2 + u
-                made.append((s, make(rows[1, s])))
-                made.append((slots + s, make(rows[0, s])))
-            for s, value in made:
-                sends[index, s] = value
-
-    def all_tiles(make, target, begin, count, group=4):
+    def send_tiles(index, which, make):
+        made = [make(rows[odd if which == 0 else 1 - odd, s]) for s in range(slots)]
+        for s, value in enumerate(made):
+            sends[index, which, s] = value
+
+    def all_tiles(make, target, begin, count, group=GROUP):
+        group = min(group, count)
+
         @pl.loop(0, count // group)
         def _(i):
             made = [make(begin + i * group + u) for u in range(group)]
             for u in range(group):
                 target[begin + i * group + u] = made[u]
 
-    for load in loads:
+    for i, load in enumerate(loads):
         load.wait()
+
+        @pl.loop(0, share // 2)
+        def _(j):
+            for u in range(2):
+                t = i * share + j * 2 + u
+                for k in range(nnz):
+                    turned[t, k * size : (k + 1) * size] = a_ref[t, k].T
+
     wait_halo(0, level0)
-    send_tiles(1, first)
-    start_halo(1, level1)
+    send_tiles(1, 0, first)
+    start_far(1, level1)
+    send_tiles(1, 1, first)
+    start_near(1, level1)
     all_tiles(first, level1, 0, tiles)
     wait_halo(1, level1)
-    send_tiles(2, second)
-    start_halo(2, level2)
+    send_tiles(2, 0, second)
+    start_far(2, level2)
+    send_tiles(2, 1, second)
+    start_near(2, level2)
 
     def exchange(c):
         span = pl.ds(c * part_rows, part_rows)
@@ -287,10 +292,11 @@
     slots = send_rows.shape[1]
     width = 2 * modes
     stages = parts.bit_length() - 1
-    assert 1 << stages == parts
+    assert 1 << stages == parts and parts > 1
     chunks = 4
     smem = pl.BlockSpec(memory_space=pltpu.SMEM)
     vmem = pl.BlockSpec(memory_space=pltpu.VMEM)
+    hbm = pl.BlockSpec(memory_space=pl.ANY)
     dma = pltpu.SemaphoreType.DMA
     level = pltpu.VMEM((tiles + 2 * slots, modes, size), jnp.bfloat16)
     field = pltpu.VMEM((tiles, modes, size), jnp.bfloat16)
@@ -300,12 +306,13 @@
             jax.ShapeDtypeStruct((modes, row_count), jnp.bfloat16),
             jax.ShapeDtypeStruct((width, width), jnp.float32),
         ),
-        in_specs=[smem, smem, smem, smem, vmem, pl.BlockSpec(memory_space=pl.ANY)],
+        in_specs=[smem, smem, smem, smem, hbm, hbm],
         out_specs=(vmem, vmem),
         scratch_shapes=[
             pltpu.VMEM(stiffness_tiles.shape, jnp.bfloat16),
-            level, level, level, field, field, field,
-            pltpu.VMEM((3, 2 * slots, modes, size), jnp.bfloat16),
+            pltpu.VMEM((tiles, nnz * size, size), jnp.bfloat16),
+            level, level, level, pltpu.VMEM((modes, row_count), jnp.bfloat16), field, field, field,
+            pltpu.VMEM((3, 2, slots, modes, size), jnp.bfloat16),
             pltpu.VMEM((stages + 1, modes, width), jnp.float32),
             pltpu.VMEM((stages + 1, modes, width), jnp.float32),
             pltpu.VMEM((width, width), jnp.float32),
@@ -314,7 +321,7 @@
             pltpu.VMEM((width, 2 * width), jnp.float32),
             pltpu.VMEM((width, width), jnp.float32),
             pltpu.VMEM((modes, width), jnp.bfloat16),
-            dma((4,)), dma((3, 2)), dma((3, 2)), dma((chunks,)), dma((chunks,)),
+            dma((1,)), dma((8,)), dma((3, 2)), dma((3, 2)), dma((chunks,)), dma((chunks,)),
             dma((stages + 2,)), dma((stages + 2,)),
         ],
         compiler_params=pltpu.CompilerParams(

time: 58.9 us -> 55.4 us (0.941)
  Pallas kernels: 53.2 us -> 49.8 us
    pallas_call x1, Pallas kernels: 53.2 us -> 49.8 us  [shards(): pl.pallas_call(functools.partial(kernel, parts), out_shape=(jax.ShapeDtyp...]
where the time goes in v1:
time: 55.4 us; the launch traced here: 55.1 us
  Pallas kernels  49.8 us (90%)
  local copies, waits for them, and re-layouts  3.34 us (6%)
  between operations  1.93 us (3%)
    pallas_call x1, Pallas kernels, shards(): pl.pallas_call(functools.partial(kernel, parts), out_shape=(jax.ShapeDtyp...  49.8 us
    unnamed x2, local copies, waits for them, and re-layouts  3.34 us

profile of v1, /device:TPU:0, one launch (start us, length us, event | category | flops | bytes accessed | tf_op | source)
XLA Modules:
  0.0 55.1 jit_solution(7314381019535078250)
XLA Ops:
  1.9 49.8 %shard_map.77 = (bf16[64,4096]{1,0:T(8,128)(2,1)}, f32[128,128]{1,0:T(8,128)}) custom-call(s32[10,32]{1,0:T(8,128)} %bitcast.5, s32[2,8]{1,0:T(2,128)} %rows.1, f32[1]{0:T(128)S(6)} %copy.10.low_ref, f32[1]{0:T(128)S(6)} %copy.11.high_ref, bf16[64,4096]{1,0:T(8,128)(2,1)} %bitcast.4, bf16[32,10,128,128]{3,2,1,0:T(8,128)(2,1)} %a_hbm.1), custom_call_target="tpu_custom_call" | custom-call | tf_op jit(solution)/shard_map/pallas_call | solution.py:303
  51.7 1.9 %copy.12 = bf16[4096,64]{0,1:T(8,128)(2,1)} copy(bf16[4096,64]{0,1:T(8,128)(2,1)} %bitcast.3) | data formatting | bytes 1048576
  53.6 1.5 %copy.13 = f32[128,128]{1,0:T(8,128)} copy(f32[128,128]{1,0:T(8,128)} %get-tuple-element.9) | data formatting | bytes 131072

commit v2 on v1

v2 whole, which is shorter than its diff:
```python
import functools

import jax
import jax.numpy as jnp
from jax import lax
from jax.experimental import pallas as pl
from jax.experimental.pallas import tpu as pltpu
from jax.sharding import PartitionSpec as P

MESH = pl.DeviceIdType.MESH
GROUP = 16
NT = (((1,), (1,)), ((), ()))
NN = (((1,), (0,)), ((), ()))
TN = (((0,), (0,)), ((), ()))
EXACT = lax.Precision.HIGHEST


def kernel(
    parts, cols, rows, low_ref, high_ref, x_hbm, a_hbm, basis_ref, ritz_ref,
    a_ref, turned, level0, level1, level2, x_ref, plain, image, other, sends,
    shares, gathered, totals, sums, work, inv_ref, inv_t,
    x_sem, a_sem, halo_send, halo_recv, mode_send, mode_recv,
    share_send, share_recv, total_send, total_recv,
):
    tiles, nnz, size = a_ref.shape[0], a_ref.shape[1], a_ref.shape[2]
    modes = x_hbm.shape[0]
    width = 2 * modes
    slots = rows.shape[1]
    chunks = mode_send.shape[0]
    p = lax.axis_index("dof")
    my = lax.axis_index("mode")
    has_low = p > 0
    has_up = p < parts - 1

    odd = lax.rem(p, 2)
    mate = p + 1 - 2 * odd
    far = p - 1 + 2 * odd
    has_far = (far >= 0) & (far < parts)
    far_slot = lax.rem(far + parts, parts)

    fetch = pltpu.make_async_copy(x_hbm, x_ref, x_sem.at[0])
    fetch.start()
    barrier = pltpu.get_barrier_semaphore()

    @pl.loop(1, 2 * parts)
    def _(d):
        peer = (lax.rem(p + d // 2, parts), lax.rem(my + d, 2))
        pl.semaphore_signal(barrier, inc=1, device_id=peer, device_id_type=MESH)

    fetch.wait()
    loads = []
    a_parts = a_sem.shape[0]
    share = tiles // a_parts
    for i in range(a_parts):
        span = pl.ds(i * share, share)
        loads.append(pltpu.make_async_copy(a_hbm.at[span], a_ref.at[span], a_sem.at[i]))
        loads[-1].start()

    for t in range(tiles):
        plain[t] = x_ref[:, t * size : (t + 1) * size]
    for s in range(slots):
        for which, row in enumerate((rows[odd, s], rows[1 - odd, s])):
            sends[0, which, s] = plain[row]

    @pl.when(p == 0)
    def _():
        for level in (level0, level1, level2):
            level[tiles : tiles + slots] = jnp.zeros((slots, modes, size), jnp.bfloat16)

    @pl.when(p == parts - 1)
    def _():
        for level in (level0, level1, level2):
            level[tiles + slots :] = jnp.zeros((slots, modes, size), jnp.bfloat16)

    pl.semaphore_wait(barrier, 2 * parts - 1)

    def halo(index, level, remote):
        hop = odd if remote else 1 - odd
        return pltpu.make_async_remote_copy(
            src_ref=sends.at[index, 0 if remote else 1],
            dst_ref=level.at[pl.ds(tiles + slots * (1 - hop), slots)],
            send_sem=halo_send.at[index, 0 if remote else 1],
            recv_sem=halo_recv.at[index, 0 if remote else 1],
            device_id=(far_slot if remote else mate, my),
            device_id_type=MESH,
        )

    def start_far(index, level):
        pl.when(has_far)(halo(index, level, True).start)

    def start_near(index, level):
        halo(index, level, False).start()

    def wait_halo(index, level):
        near, remote = halo(index, level, False), halo(index, level, True)
        near.wait_recv()
        near.wait_send()
        pl.when(has_far)(remote.wait_recv)
        pl.when(has_far)(remote.wait_send)

    start_far(0, level0)
    start_near(0, level0)
    for t in range(tiles):
        level0[t] = plain[t]

    center = (high_ref[0] + low_ref[0]) * 0.5
    half_width = (high_ref[0] - low_ref[0]) * 0.5
    scale = jnp.ones((1, size), jnp.float32) / jnp.full((1, size), half_width, jnp.float32)

    def product(level, t):
        field = jnp.concatenate([level[cols[k, t]] for k in range(nnz)], axis=1)
        return lax.dot_general(field, turned[t], NN, preferred_element_type=jnp.float32)

    def first(t):
        own = level0[t].astype(jnp.float32)
        return ((product(level0, t) - center * own) * scale).astype(jnp.bfloat16)

    def second(t):
        own = level1[t].astype(jnp.float32)
        before = level0[t].astype(jnp.float32)
        return (2.0 * (product(level1, t) - center * own) * scale - before).astype(jnp.bfloat16)

    def send_tiles(index, which, make):
        made = [make(rows[odd if which == 0 else 1 - odd, s]) for s in range(slots)]
        for s, value in enumerate(made):
            sends[index, which, s] = value

    def all_tiles(make, target, begin, count, group=GROUP):
        group = min(group, count)

        @pl.loop(0, count // group)
        def _(i):
            made = [make(begin + i * group + u) for u in range(group)]
            for u in range(group):
                target[begin + i * group + u] = made[u]

    for i, load in enumerate(loads):
        load.wait()

        @pl.loop(0, share // 2)
        def _(j):
            for u in range(2):
                t = i * share + j * 2 + u
                for k in range(nnz):
                    turned[t, k * size : (k + 1) * size] = a_ref[t, k].T

    wait_halo(0, level0)
    send_tiles(1, 0, first)
    start_far(1, level1)
    send_tiles(1, 1, first)
    start_near(1, level1)
    all_tiles(first, level1, 0, tiles)
    wait_halo(1, level1)
    half = tiles // 2
    quarter = half // 4
    pieces = [(0, quarter), (quarter, quarter), (2 * quarter, 2 * quarter)]
    pieces = [(0, *piece) for piece in pieces] + [(1, 0, half // 2), (1, half // 2, half // 2)]
    urgent = range(3)
    later = range(3, 5)

    def exchange(c, sender):
        which, offset, count = pieces[c]
        begin = (sender if which == 0 else 1 - sender) * half + offset
        span = pl.ds(begin, count)
        return pltpu.make_async_remote_copy(
            src_ref=level2.at[span],
            dst_ref=other.at[span],
            send_sem=mode_send.at[c],
            recv_sem=mode_recv.at[c],
            device_id=(p, 1 - my),
            device_id_type=MESH,
        )

    def exchanged(c):
        which, offset, count = pieces[c]
        begin = (my if which == 0 else 1 - my) * half + offset
        all_tiles(second, level2, begin, count)
        exchange(c, my).start()

    block = shares.shape[2]
    base = (parts - 8) // 2

    def owners(k):
        return [base + k + 2 * b for b in range(4)] if k < 2 else [base + b for b in range(8)]

    def owned(k):
        place = p - base
        inside = (place >= 0) & (place < 8)
        return inside & (lax.rem(place + 8, 2) == k) if k < 2 else inside

    def blocks_wait(ref, count, sem):
        view = ref.at[pl.ds(0, count)]
        pltpu.make_async_copy(view, view, sem).wait()

    def share(k, value):
        for b, owner in enumerate(owners(k)):
            shares[k, b] = value[b * block : (b + 1) * block]
        for b, owner in enumerate(owners(k)):
            copy = pltpu.make_async_remote_copy(
                src_ref=shares.at[k, b],
                dst_ref=gathered.at[k * parts + p],
                send_sem=share_send.at[k],
                recv_sem=share_recv.at[k],
                device_id=(owner, my),
                device_id_type=MESH,
            )
            pl.when(p != owner)(copy.start)

            @pl.when(p == owner)
            def _():
                gathered[k * parts + p] = shares[k, b]

    def total(k):
        count = len(owners(k))

        @pl.when(owned(k))
        def _():
            blocks_wait(gathered, parts - 1, share_recv.at[k])
            value = gathered[k * parts]
            for q in range(1, parts):
                value = value + gathered[k * parts + q]
            sums[k] = value
            slot = my * count + (p - base) // (8 // count)
            totals[k, slot] = value

            @pl.loop(1, 2 * parts)
            def _(d):
                pltpu.make_async_remote_copy(
                    src_ref=sums.at[k],
                    dst_ref=totals.at[k, slot],
                    send_sem=total_send.at[k],
                    recv_sem=total_recv.at[k],
                    device_id=(lax.rem(p + d // 2, parts), lax.rem(my + d, 2)),
                    device_id_type=MESH,
                ).start()

    def arrived(k):
        count = len(owners(k))

        @pl.when(owned(k))
        def _():
            blocks_wait(totals.at[k], 2 * count - 1, total_recv.at[k])

        @pl.when(jnp.logical_not(owned(k)))
        def _():
            blocks_wait(totals.at[k], 2 * count, total_recv.at[k])

        flat = totals[k, : 2 * count].reshape(2, count * block, width) / (parts * tiles * size)
        return flat[0], flat[1]

    def sent(k):
        count = len(owners(k))

        @pl.when(owned(k))
        def _():
            blocks_wait(shares.at[k], count - 1, share_send.at[k])
            blocks_wait(gathered, 2 * parts - 1, total_send.at[k])

        @pl.when(jnp.logical_not(owned(k)))
        def _():
            blocks_wait(shares.at[k], count, share_send.at[k])

    def contract(left, right, begin, count):
        acc = jnp.zeros((modes, modes), jnp.float32)
        for i in range(0, count, 8):
            lhs = jnp.concatenate([left[begin + i + u] for u in range(8)], axis=1)
            rhs = jnp.concatenate([right[begin + i + u] for u in range(8)], axis=1)
            acc = acc + lax.dot_general(lhs, rhs, NT, preferred_element_type=jnp.float32)
        return acc

    def fold(value):
        return jnp.concatenate([value[: modes // 2], value[modes // 2 :]], axis=1)

    def unfold(value):
        return jnp.concatenate([value[:, :modes], value[:, modes:]], axis=0)

    for c in urgent:
        exchanged(c)
    send_tiles(2, 0, second)
    start_far(2, level2)
    send_tiles(2, 1, second)
    start_near(2, level2)
    for c in later:
        exchanged(c)
    share(0, fold(contract(level2, level2, 0, tiles)))
    wait_halo(2, level2)
    all_tiles(lambda t: product(level2, t).astype(jnp.bfloat16), image, 0, tiles)
    for c in urgent:
        exchange(c, 1 - my).wait_recv()
    cross = contract(level2, other, (1 - my) * half, half)
    share(1, fold(jnp.where(my == 0, cross, cross.T)))
    total(0)
    own_projected = contract(image, level2, 0, tiles)
    mixed = contract(image, other, (1 - my) * half, half)
    total(1)
    for c in later:
        exchange(c, 1 - my).wait_recv()
    mixed = mixed + contract(image, other, my * half, half)
    pair = jnp.concatenate([own_projected, mixed], axis=1)
    share(2, jnp.where(my == 0, pair, pltpu.roll(pair, modes, 1)))

    step = 16
    row_id = lax.broadcasted_iota(jnp.int32, (modes, modes), 0)
    col_id = lax.broadcasted_iota(jnp.int32, (modes, modes), 1)
    small = lax.broadcasted_iota(jnp.int32, (step, 1), 0)
    lanes = lax.broadcasted_iota(jnp.int32, (step, width), 1)

    def exact(left, right, dims):
        return lax.dot_general(
            left, right, dims, precision=EXACT, preferred_element_type=jnp.float32
        )

    def factor_inverse(gram):
        eye = (row_id == col_id).astype(jnp.float32)
        work[...] = jnp.concatenate([gram, eye], axis=1)

        @pl.loop(0, modes // step)
        def _(b):
            begin = pl.multiple_of(b * step, step)
            panel = work[pl.ds(begin, step), :]
            near = panel
            columns = [
                jnp.sum(jnp.where(lanes == begin + s, near, 0.0), axis=1, keepdims=True)
                for s in range(step)
            ]
            pivots = jnp.zeros((step, 1), jnp.float32)
            for q in range(step):
                pivot = columns[q][q : q + 1, :]
                pivots = jnp.where(small == q, pivot, pivots)
                if q == step - 1:
                    break
                factor = jnp.where(small > q, columns[q] / pivot, 0.0)
                panel = panel - factor * panel[q : q + 1, :]
                for s in range(q + 1, step):
                    columns[s] = columns[s] - factor * columns[s][q : q + 1, :]
            inv_ref[pl.ds(begin, step), :] = panel / jnp.sqrt(pivots)
            ahead = (lanes >= begin + step) & (lanes < modes)
            below = jnp.where(ahead, panel / pivots, 0.0)[:, :modes]
            work[...] = work[...] - exact(below, panel, TN)

        return inv_ref[...][:, modes:]

    gram0, gram1 = arrived(0)
    gram0, gram1 = unfold(gram0), unfold(gram1)
    inv00 = factor_inverse(gram0)
    cross0, cross1 = arrived(1)
    bridge = exact(inv00, unfold(cross0 + cross1), NN)
    rest = gram1 - exact(bridge, bridge, TN)
    turn = exact(bridge, inv00, TN)
    total(2)
    inv11 = factor_inverse(rest)
    inv10 = -exact(inv11, turn, NN)
    lower = jnp.concatenate([inv10, inv11], axis=1)
    upper = jnp.concatenate([inv00, jnp.zeros((modes, modes), jnp.float32)], axis=1)
    inverse = jnp.concatenate([upper, lower], axis=0)
    own = jnp.where(my == 0, upper, pltpu.roll(lower, modes, 1))
    inv_t[...] = own.astype(jnp.bfloat16)
    for t in range(0, tiles, 2):
        two = jnp.concatenate(
            [jnp.concatenate([level2[u], other[u]], axis=0) for u in (t, t + 1)], axis=1
        )
        basis_ref[:, t * size : (t + 2) * size] = lax.dot_general(
            inv_t[...], two, NN, preferred_element_type=jnp.float32
        ).astype(jnp.bfloat16)
    projected0, projected1 = arrived(2)
    projected_t = jnp.concatenate([projected0, projected1], axis=0)
    ritz_ref[...] = exact(exact(inverse, projected_t, NT), inverse, NT)
    for c in range(chunks):
        exchange(c, my).wait_send()
    for k in range(3):
        sent(k)


def shards(parts, stiffness_tiles, tile_cols, send_rows, block, lower_bound, upper_bound):
    row_count, modes = block.shape
    tiles, nnz, size = stiffness_tiles.shape[:3]
    slots = send_rows.shape[1]
    width = 2 * modes
    assert parts >= 16 and parts % 2 == 0
    chunks = 5
    smem = pl.BlockSpec(memory_space=pltpu.SMEM)
    vmem = pl.BlockSpec(memory_space=pltpu.VMEM)
    hbm = pl.BlockSpec(memory_space=pl.ANY)
    dma = pltpu.SemaphoreType.DMA
    level = pltpu.VMEM((tiles + 2 * slots, modes, size), jnp.bfloat16)
    field = pltpu.VMEM((tiles, modes, size), jnp.bfloat16)
    basis, ritz = pl.pallas_call(
        functools.partial(kernel, parts),
        out_shape=(
            jax.ShapeDtypeStruct((modes, row_count), jnp.bfloat16),
            jax.ShapeDtypeStruct((width, width), jnp.float32),
        ),
        in_specs=[smem, smem, smem, smem, hbm, hbm],
        out_specs=(vmem, vmem),
        scratch_shapes=[
            pltpu.VMEM(stiffness_tiles.shape, jnp.bfloat16),
            pltpu.VMEM((tiles, nnz * size, size), jnp.bfloat16),
            level, level, level, pltpu.VMEM((modes, row_count), jnp.bfloat16), field, field, field,
            pltpu.VMEM((3, 2, slots, modes, size), jnp.bfloat16),
            pltpu.VMEM((3, 8, 8, width), jnp.float32),
            pltpu.VMEM((3 * parts, 8, width), jnp.float32),
            pltpu.VMEM((3, 16, 8, width), jnp.float32),
            pltpu.VMEM((3, 8, width), jnp.float32),
            pltpu.VMEM((modes, width), jnp.float32),
            pltpu.VMEM((modes, width), jnp.float32),
            pltpu.VMEM((modes, width), jnp.bfloat16),
            dma((1,)), dma((8,)), dma((3, 2)), dma((3, 2)), dma((chunks,)), dma((chunks,)),
            dma((3,)), dma((3,)), dma((3,)), dma((3,)),
        ],
        compiler_params=pltpu.CompilerParams(
            collective_id=0, has_side_effects=True, vmem_limit_bytes=60 * 1024 * 1024
        ),
    )(tile_cols.T, send_rows, lower_bound, upper_bound, block.T, stiffness_tiles)
    return basis.T, ritz


def solution(mesh):
    placed = (
        P("dof", None, None, None),
        P("dof", None),
        P("dof", None),
        P("dof", "mode"),
        P(),
        P(),
    )
    return jax.shard_map(
        functools.partial(shards, mesh.shape["dof"]),
        mesh=mesh, in_specs=placed, out_specs=(P("dof", "mode"), P()), check_vma=False,
    )
```

time: 55.4 us -> 46.3 us (0.84)
  Pallas kernels: 49.8 us -> 40.7 us
    pallas_call x1, Pallas kernels: 49.8 us -> 40.7 us  [shards(): pl.pallas_call(functools.partial(kernel, parts), out_shape=(jax.ShapeDtyp...]
where the time goes in v2:
time: 46.3 us; the launch traced here: 46 us
  Pallas kernels  40.7 us (88%)
  local copies, waits for them, and re-layouts  3.34 us (7%)
  between operations  1.93 us (4%)
    pallas_call x1, Pallas kernels, shards(): pl.pallas_call(functools.partial(kernel, parts), out_shape=(jax.ShapeDtyp...  40.7 us
    unnamed x2, local copies, waits for them, and re-layouts  3.34 us

profile of v2, /device:TPU:0, one launch (start us, length us, event | category | flops | bytes accessed | tf_op | source)
XLA Modules:
  0.0 46.0 jit_solution(13545584591871378904)
XLA Ops:
  1.9 40.7 %shard_map.77 = (bf16[64,4096]{1,0:T(8,128)(2,1)}, f32[128,128]{1,0:T(8,128)}) custom-call(s32[10,32]{1,0:T(8,128)} %bitcast.5, s32[2,8]{1,0:T(2,128)} %rows.1, f32[1]{0:T(128)S(6)} %copy.10.low_ref, f32[1]{0:T(128)S(6)} %copy.11.high_ref, bf16[64,4096]{1,0:T(8,128)(2,1)} %bitcast.4, bf16[32,10,128,128]{3,2,1,0:T(8,128)(2,1)} %a_hbm.1), custom_call_target="tpu_custom_call" | custom-call | tf_op jit(solution)/shard_map/pallas_call | solution.py:387
  42.6 1.9 %copy.12 = bf16[4096,64]{0,1:T(8,128)(2,1)} copy(bf16[4096,64]{0,1:T(8,128)(2,1)} %bitcast.3) | data formatting | bytes 1048576
  44.5 1.5 %copy.13 = f32[128,128]{1,0:T(8,128)} copy(f32[128,128]{1,0:T(8,128)} %get-tuple-element.9) | data formatting | bytes 131072

commit v3 on v2

--- a/solution.py
+++ b/solution.py
@@ -16,16 +16,18 @@
 
 
 def kernel(
-    parts, cols, rows, low_ref, high_ref, x_hbm, a_hbm, basis_ref, ritz_ref,
+    parts, cols_hbm, rows_hbm, low_hbm, high_hbm, x_hbm, a_hbm, fields_ref, inv_t, ritz_ref,
     a_ref, turned, level0, level1, level2, x_ref, plain, image, other, sends,
-    shares, gathered, totals, sums, work, inv_ref, inv_t,
-    x_sem, a_sem, halo_send, halo_recv, mode_send, mode_recv,
+    shares, gathered, totals, sums, work, inv_ref,
+    cols, rows, low_ref, high_ref, x_sem, a_sem, keep_sem, halo_send, halo_recv, mode_send, mode_recv,
     share_send, share_recv, total_send, total_recv,
 ):
     tiles, nnz, size = a_ref.shape[0], a_ref.shape[1], a_ref.shape[2]
     modes = x_hbm.shape[0]
     width = 2 * modes
     slots = rows.shape[1]
+    tables = [(cols_hbm, cols), (rows_hbm, rows), (low_hbm, low_ref), (high_hbm, high_ref)]
+    tables = [pltpu.make_async_copy(*pair, x_sem.at[1 + i]) for i, pair in enumerate(tables)]
     chunks = mode_send.shape[0]
     p = lax.axis_index("dof")
     my = lax.axis_index("mode")
@@ -40,6 +42,8 @@
 
     fetch = pltpu.make_async_copy(x_hbm, x_ref, x_sem.at[0])
     fetch.start()
+    for table in tables:
+        table.start()
     barrier = pltpu.get_barrier_semaphore()
 
     @pl.loop(1, 2 * parts)
@@ -55,6 +59,8 @@
         span = pl.ds(i * share, share)
         loads.append(pltpu.make_async_copy(a_hbm.at[span], a_ref.at[span], a_sem.at[i]))
         loads[-1].start()
+    for table in tables:
+        table.wait()
 
     for t in range(tiles):
         plain[t] = x_ref[:, t * size : (t + 1) * size]
@@ -282,6 +288,8 @@
     start_near(2, level2)
     for c in later:
         exchanged(c)
+    keep_own = pltpu.make_async_copy(level2.at[pl.ds(0, tiles)], fields_ref.at[0], keep_sem.at[0])
+    keep_own.start()
     share(0, fold(contract(level2, level2, 0, tiles)))
     wait_halo(2, level2)
     all_tiles(lambda t: product(level2, t).astype(jnp.bfloat16), image, 0, tiles)
@@ -295,6 +303,8 @@
     total(1)
     for c in later:
         exchange(c, 1 - my).wait_recv()
+    keep_other = pltpu.make_async_copy(other, fields_ref.at[1], keep_sem.at[1])
+    keep_other.start()
     mixed = mixed + contract(image, other, my * half, half)
     pair = jnp.concatenate([own_projected, mixed], axis=1)
     share(2, jnp.where(my == 0, pair, pltpu.roll(pair, modes, 1)))
@@ -355,20 +365,27 @@
     inverse = jnp.concatenate([upper, lower], axis=0)
     own = jnp.where(my == 0, upper, pltpu.roll(lower, modes, 1))
     inv_t[...] = own.astype(jnp.bfloat16)
-    for t in range(0, tiles, 2):
-        two = jnp.concatenate(
-            [jnp.concatenate([level2[u], other[u]], axis=0) for u in (t, t + 1)], axis=1
-        )
-        basis_ref[:, t * size : (t + 2) * size] = lax.dot_general(
-            inv_t[...], two, NN, preferred_element_type=jnp.float32
-        ).astype(jnp.bfloat16)
     projected0, projected1 = arrived(2)
     projected_t = jnp.concatenate([projected0, projected1], axis=0)
     ritz_ref[...] = exact(exact(inverse, projected_t, NT), inverse, NT)
+    keep_own.wait()
+    keep_other.wait()
     for c in range(chunks):
         exchange(c, my).wait_send()
     for k in range(3):
         sent(k)
+
+
+def finish(fields, inv_t, ritz_in, basis_ref, ritz_ref):
+    tiles, size = fields.shape[1], fields.shape[3]
+    ritz_ref[...] = ritz_in[...]
+    for t in range(0, tiles, 2):
+        pair = jnp.concatenate(
+            [jnp.concatenate([fields[0, u], fields[1, u]], axis=0) for u in (t, t + 1)], axis=1
+        )
+        basis_ref[:, t * size : (t + 2) * size] = lax.dot_general(
+            inv_t[...], pair, NN, preferred_element_type=jnp.float32
+        ).astype(jnp.bfloat16)
 
 
 def shards(parts, stiffness_tiles, tile_cols, send_rows, block, lower_bound, upper_bound):
@@ -378,20 +395,21 @@
     width = 2 * modes
     assert parts >= 16 and parts % 2 == 0
     chunks = 5
-    smem = pl.BlockSpec(memory_space=pltpu.SMEM)
     vmem = pl.BlockSpec(memory_space=pltpu.VMEM)
     hbm = pl.BlockSpec(memory_space=pl.ANY)
+    far = pl.BlockSpec(memory_space=pltpu.HBM)
     dma = pltpu.SemaphoreType.DMA
     level = pltpu.VMEM((tiles + 2 * slots, modes, size), jnp.bfloat16)
     field = pltpu.VMEM((tiles, modes, size), jnp.bfloat16)
-    basis, ritz = pl.pallas_call(
+    fields, inv_t, ritz = pl.pallas_call(
         functools.partial(kernel, parts),
         out_shape=(
-            jax.ShapeDtypeStruct((modes, row_count), jnp.bfloat16),
+            jax.ShapeDtypeStruct((2, tiles, modes, size), jnp.bfloat16),
+            jax.ShapeDtypeStruct((modes, width), jnp.bfloat16),
             jax.ShapeDtypeStruct((width, width), jnp.float32),
         ),
-        in_specs=[smem, smem, smem, smem, hbm, hbm],
-        out_specs=(vmem, vmem),
+        in_specs=[far] * 6,
+        out_specs=(hbm, vmem, vmem),
         scratch_shapes=[
             pltpu.VMEM(stiffness_tiles.shape, jnp.bfloat16),
             pltpu.VMEM((tiles, nnz * size, size), jnp.bfloat16),
@@ -403,14 +421,31 @@
             pltpu.VMEM((3, 8, width), jnp.float32),
             pltpu.VMEM((modes, width), jnp.float32),
             pltpu.VMEM((modes, width), jnp.float32),
-            pltpu.VMEM((modes, width), jnp.bfloat16),
-            dma((1,)), dma((8,)), dma((3, 2)), dma((3, 2)), dma((chunks,)), dma((chunks,)),
+            pltpu.SMEM((nnz, tiles), jnp.int32),
+            pltpu.SMEM(send_rows.shape, jnp.int32),
+            pltpu.SMEM((1,), jnp.float32),
+            pltpu.SMEM((1,), jnp.float32),
+            dma((5,)), dma((8,)), dma((2,)), dma((3, 2)), dma((3, 2)), dma((chunks,)), dma((chunks,)),
             dma((3,)), dma((3,)), dma((3,)), dma((3,)),
         ],
         compiler_params=pltpu.CompilerParams(
-            collective_id=0, has_side_effects=True, vmem_limit_bytes=60 * 1024 * 1024
+            collective_id=0, has_side_effects=True, vmem_limit_bytes=50331648
         ),
-    )(tile_cols.T, send_rows, lower_bound, upper_bound, block.T, stiffness_tiles)
+    )(
+        *[pltpu.with_memory_space_constraint(ref, pltpu.HBM) for ref in (tile_cols.T, send_rows)],
+        lower_bound, upper_bound,
+        *[pltpu.with_memory_space_constraint(ref, pltpu.HBM) for ref in (block.T, stiffness_tiles)],
+    )
+    basis, ritz = pl.pallas_call(
+        finish,
+        out_shape=(
+            jax.ShapeDtypeStruct((modes, row_count), jnp.bfloat16),
+            jax.ShapeDtypeStruct((width, width), jnp.float32),
+        ),
+        in_specs=[vmem, vmem, vmem],
+        out_specs=(vmem, vmem),
+        compiler_params=pltpu.CompilerParams(vmem_limit_bytes=8 * 1024 * 1024),
+    )(fields, inv_t, ritz)
     return basis.T, ritz
 
 

time: 46.3 us -> 42.3 us (0.914)
  local copies, waits for them, and re-layouts: 3.34 us -> 0 us
  Pallas kernels: 40.7 us -> 40.2 us
    unnamed x2 -> x0, local copies, waits for them, and re-layouts: 3.34 us -> none
    pallas_call x1, Pallas kernels: 40.7 us -> 39.1 us  [shards(): pl.pallas_call(functools.partial(kernel, parts), out_shape=(jax.ShapeDtyp...]
    pallas_call x0 -> x1, Pallas kernels: none -> 1.1 us  [shards(): pl.pallas_call(finish, out_shape=(jax.ShapeDtypeStruct((modes, row_count)...]
where the time goes in v3:
time: 42.3 us; the launch traced here: 42.1 us
  Pallas kernels  40.2 us (95%)
  between operations  1.93 us (5%)
    pallas_call x1, Pallas kernels, shards(): pl.pallas_call(functools.partial(kernel, parts), out_shape=(jax.ShapeDtyp...  39.1 us
    pallas_call x1, Pallas kernels, shards(): pl.pallas_call(finish, out_shape=(jax.ShapeDtypeStruct((modes, row_count)...  1.1 us

profile of v3, /device:TPU:0, one launch (start us, length us, event | category | flops | bytes accessed | tf_op | source)
XLA Modules:
  0.0 42.1 jit_solution(15971304607053216751)
XLA Ops:
  1.9 39.1 %shard_map.77 = (bf16[2,32,64,128]{3,2,1,0:T(8,128)(2,1)S(1)}, bf16[64,128]{1,0:T(8,128)(2,1)S(1)}, f32[128,128]{1,0:T(8,128)S(1)}) custom-call(s32[10,32]{1,0:T(8,128)} %bitcast.4, s32[2,8]{1,0:T(2,128)} %rows_hbm.1, f32[1]{0:T(128)S(6)} %copy.8.low_hbm, f32[1]{0:T(128)S(6)} %copy.9.high_hbm, bf16[64,4096]{1,0:T(8,128)(2,1)} %bitcast.3, ...), custom_call_target="tpu_custom_call" | custom-call | tf_op jit(solution)/shard_map/pallas_call | solution.py:404
  41.0 1.1 %shard_map.78 = (bf16[64,4096]{1,0:T(8,128)(2,1)}, f32[128,128]{1,0:T(8,128)}) custom-call(bf16[2,32,64,128]{3,2,1,0:T(8,128)(2,1)S(1)} %get-tuple-element.7.fields, bf16[64,128]{1,0:T(8,128)(2,1)S(1)} %get-tuple-element.8.inv_t, f32[128,128]{1,0:T(8,128)S(1)} %get-tuple-element.9.ritz_in), custom_call_target="tpu_custom_call" | custom-call | tf_op jit(solution)/shard_map/pallas_call | solution.py:439

commit v4 on v3

--- a/solution.py
+++ b/solution.py
@@ -16,9 +16,9 @@
 
 
 def kernel(
-    parts, cols_hbm, rows_hbm, low_hbm, high_hbm, x_hbm, a_hbm, fields_ref, inv_t, ritz_ref,
+    parts, cols_hbm, rows_hbm, low_hbm, high_hbm, x_hbm, a_hbm, basis_ref, ritz_ref,
     a_ref, turned, level0, level1, level2, x_ref, plain, image, other, sends,
-    shares, gathered, totals, sums, work, inv_ref,
+    shares, gathered, totals, sums, work, inv_ref, inv_t, basis,
     cols, rows, low_ref, high_ref, x_sem, a_sem, keep_sem, halo_send, halo_recv, mode_send, mode_recv,
     share_send, share_recv, total_send, total_recv,
 ):
@@ -44,21 +44,32 @@
     fetch.start()
     for table in tables:
         table.start()
-    barrier = pltpu.get_barrier_semaphore()
-
-    @pl.loop(1, 2 * parts)
-    def _(d):
-        peer = (lax.rem(p + d // 2, parts), lax.rem(my + d, 2))
-        pl.semaphore_signal(barrier, inc=1, device_id=peer, device_id_type=MESH)
-
-    fetch.wait()
     loads = []
     a_parts = a_sem.shape[0]
-    share = tiles // a_parts
+    span = tiles // a_parts
     for i in range(a_parts):
-        span = pl.ds(i * share, share)
-        loads.append(pltpu.make_async_copy(a_hbm.at[span], a_ref.at[span], a_sem.at[i]))
-        loads[-1].start()
+        view = pl.ds(i * span, span)
+        loads.append(pltpu.make_async_copy(a_hbm.at[view], a_ref.at[view], a_sem.at[i]))
+    for load in loads[:2]:
+        load.start()
+
+    def peer(shift, other_mode):
+        place = p + shift
+        place = jnp.where(place >= parts, place - parts, place)
+        return place, 1 - my if other_mode else my
+
+    near_first = sorted(
+        ((d, e) for d in range(parts) for e in range(2) if d or e),
+        key=lambda pair: (min(pair[0], parts - pair[0]), pair[1]),
+    )
+    barrier = pltpu.get_barrier_semaphore()
+    for shift, other_mode in near_first:
+        pl.semaphore_signal(
+            barrier, inc=1, device_id=peer(shift, other_mode), device_id_type=MESH
+        )
+    fetch.wait()
+    for load in loads[2:]:
+        load.start()
     for table in tables:
         table.wait()
 
@@ -80,31 +91,36 @@
 
     pl.semaphore_wait(barrier, 2 * parts - 1)
 
-    def halo(index, level, remote):
-        hop = odd if remote else 1 - odd
+    def halo(index, level, which):
+        hop = 1 - odd if which == 2 else odd
+        count = slots if which == 2 else slots // 2
+        first_slot = slots // 2 if which == 1 else 0
         return pltpu.make_async_remote_copy(
-            src_ref=sends.at[index, 0 if remote else 1],
-            dst_ref=level.at[pl.ds(tiles + slots * (1 - hop), slots)],
-            send_sem=halo_send.at[index, 0 if remote else 1],
-            recv_sem=halo_recv.at[index, 0 if remote else 1],
-            device_id=(far_slot if remote else mate, my),
+            src_ref=sends.at[index, which // 2, pl.ds(first_slot, count)],
+            dst_ref=level.at[pl.ds(tiles + slots * (1 - hop) + first_slot, count)],
+            send_sem=halo_send.at[index, which],
+            recv_sem=halo_recv.at[index, which],
+            device_id=(mate if which == 2 else far_slot, my),
             device_id_type=MESH,
         )
 
-    def start_far(index, level):
-        pl.when(has_far)(halo(index, level, True).start)
+    def start_far(index, level, which):
+        pl.when(has_far)(halo(index, level, which).start)
 
     def start_near(index, level):
-        halo(index, level, False).start()
+        halo(index, level, 2).start()
 
     def wait_halo(index, level):
-        near, remote = halo(index, level, False), halo(index, level, True)
+        near = halo(index, level, 2)
         near.wait_recv()
         near.wait_send()
-        pl.when(has_far)(remote.wait_recv)
-        pl.when(has_far)(remote.wait_send)
-
-    start_far(0, level0)
+        for which in range(2):
+            copy = halo(index, level, which)
+            pl.when(has_far)(copy.wait_recv)
+            pl.when(has_far)(copy.wait_send)
+
+    start_far(0, level0, 0)
+    start_far(0, level0, 1)
     start_near(0, level0)
     for t in range(tiles):
         level0[t] = plain[t]
@@ -126,10 +142,17 @@
         before = level0[t].astype(jnp.float32)
         return (2.0 * (product(level1, t) - center * own) * scale - before).astype(jnp.bfloat16)
 
-    def send_tiles(index, which, make):
-        made = [make(rows[odd if which == 0 else 1 - odd, s]) for s in range(slots)]
-        for s, value in enumerate(made):
-            sends[index, which, s] = value
+    def send_tiles(index, level, make):
+        for which in range(2):
+            begin = which * (slots // 2)
+            made = [make(rows[odd, begin + u]) for u in range(slots // 2)]
+            for u, value in enumerate(made):
+                sends[index, 0, begin + u] = value
+            start_far(index, level, which)
+        made = [make(rows[1 - odd, u]) for u in range(slots)]
+        for u, value in enumerate(made):
+            sends[index, 1, u] = value
+        start_near(index, level)
 
     def all_tiles(make, target, begin, count, group=GROUP):
         group = min(group, count)
@@ -143,18 +166,15 @@
     for i, load in enumerate(loads):
         load.wait()
 
-        @pl.loop(0, share // 2)
+        @pl.loop(0, span // 2)
         def _(j):
             for u in range(2):
-                t = i * share + j * 2 + u
+                t = i * span + j * 2 + u
                 for k in range(nnz):
                     turned[t, k * size : (k + 1) * size] = a_ref[t, k].T
 
     wait_halo(0, level0)
-    send_tiles(1, 0, first)
-    start_far(1, level1)
-    send_tiles(1, 1, first)
-    start_near(1, level1)
+    send_tiles(1, level1, first)
     all_tiles(first, level1, 0, tiles)
     wait_halo(1, level1)
     half = tiles // 2
@@ -187,12 +207,12 @@
     base = (parts - 8) // 2
 
     def owners(k):
-        return [base + k + 2 * b for b in range(4)] if k < 2 else [base + b for b in range(8)]
+        return [base + b for b in range(8)] if k == 2 else [base + k % 2 + 2 * b for b in range(4)]
 
     def owned(k):
         place = p - base
         inside = (place >= 0) & (place < 8)
-        return inside & (lax.rem(place + 8, 2) == k) if k < 2 else inside
+        return inside if k == 2 else inside & (lax.rem(p - base + parts, 2) == k % 2)
 
     def blocks_wait(ref, count, sem):
         view = ref.at[pl.ds(0, count)]
@@ -229,14 +249,13 @@
             slot = my * count + (p - base) // (8 // count)
             totals[k, slot] = value
 
-            @pl.loop(1, 2 * parts)
-            def _(d):
+            for shift, other_mode in reversed(near_first):
                 pltpu.make_async_remote_copy(
                     src_ref=sums.at[k],
                     dst_ref=totals.at[k, slot],
                     send_sem=total_send.at[k],
                     recv_sem=total_recv.at[k],
-                    device_id=(lax.rem(p + d // 2, parts), lax.rem(my + d, 2)),
+                    device_id=peer(shift, other_mode),
                     device_id_type=MESH,
                 ).start()
 
@@ -282,14 +301,9 @@
 
     for c in urgent:
         exchanged(c)
-    send_tiles(2, 0, second)
-    start_far(2, level2)
-    send_tiles(2, 1, second)
-    start_near(2, level2)
+    send_tiles(2, level2, second)
     for c in later:
         exchanged(c)
-    keep_own = pltpu.make_async_copy(level2.at[pl.ds(0, tiles)], fields_ref.at[0], keep_sem.at[0])
-    keep_own.start()
     share(0, fold(contract(level2, level2, 0, tiles)))
     wait_halo(2, level2)
     all_tiles(lambda t: product(level2, t).astype(jnp.bfloat16), image, 0, tiles)
@@ -300,14 +314,15 @@
     total(0)
     own_projected = contract(image, level2, 0, tiles)
     mixed = contract(image, other, (1 - my) * half, half)
-    total(1)
-    for c in later:
-        exchange(c, 1 - my).wait_recv()
-    keep_other = pltpu.make_async_copy(other, fields_ref.at[1], keep_sem.at[1])
-    keep_other.start()
-    mixed = mixed + contract(image, other, my * half, half)
     pair = jnp.concatenate([own_projected, mixed], axis=1)
     share(2, jnp.where(my == 0, pair, pltpu.roll(pair, modes, 1)))
+    total(1)
+    total(2)
+    rest_begin = my * half
+    exchange(3, 1 - my).wait_recv()
+    mixed = contract(image, other, rest_begin, half // 2)
+    exchange(4, 1 - my).wait_recv()
+    share(3, fold(mixed + contract(image, other, rest_begin + half // 2, half // 2)))
 
     step = 16
     row_id = lax.broadcasted_iota(jnp.int32, (modes, modes), 0)
@@ -357,35 +372,50 @@
     bridge = exact(inv00, unfold(cross0 + cross1), NN)
     rest = gram1 - exact(bridge, bridge, TN)
     turn = exact(bridge, inv00, TN)
-    total(2)
+    total(3)
     inv11 = factor_inverse(rest)
     inv10 = -exact(inv11, turn, NN)
     lower = jnp.concatenate([inv10, inv11], axis=1)
-    upper = jnp.concatenate([inv00, jnp.zeros((modes, modes), jnp.float32)], axis=1)
+    blank = jnp.zeros((modes, modes), jnp.float32)
+    upper = jnp.concatenate([inv00, blank], axis=1)
     inverse = jnp.concatenate([upper, lower], axis=0)
     own = jnp.where(my == 0, upper, pltpu.roll(lower, modes, 1))
     inv_t[...] = own.astype(jnp.bfloat16)
-    projected0, projected1 = arrived(2)
-    projected_t = jnp.concatenate([projected0, projected1], axis=0)
+    for t in range(0, tiles, 2):
+        two = jnp.concatenate(
+            [jnp.concatenate([level2[u], other[u]], axis=0) for u in (t, t + 1)], axis=1
+        )
+        basis[:, t * size : (t + 2) * size] = lax.dot_general(
+            inv_t[...], two, NN, preferred_element_type=jnp.float32
+        ).astype(jnp.bfloat16)
+    keep = pltpu.make_async_copy(basis, basis_ref, keep_sem.at[0])
+    keep.start()
+    projected_t = jnp.concatenate(arrived(2), axis=0)
+    late0, late1 = arrived(3)
+    projected_t = projected_t + jnp.concatenate(
+        [
+            jnp.concatenate([blank, unfold(late0)], axis=1),
+            jnp.concatenate([unfold(late1), blank], axis=1),
+        ],
+        axis=0,
+    )
     ritz_ref[...] = exact(exact(inverse, projected_t, NT), inverse, NT)
-    keep_own.wait()
-    keep_other.wait()
+    keep.wait()
     for c in range(chunks):
         exchange(c, my).wait_send()
-    for k in range(3):
+    for k in range(4):
         sent(k)
 
 
-def finish(fields, inv_t, ritz_in, basis_ref, ritz_ref):
-    tiles, size = fields.shape[1], fields.shape[3]
-    ritz_ref[...] = ritz_in[...]
-    for t in range(0, tiles, 2):
-        pair = jnp.concatenate(
-            [jnp.concatenate([fields[0, u], fields[1, u]], axis=0) for u in (t, t + 1)], axis=1
-        )
-        basis_ref[:, t * size : (t + 2) * size] = lax.dot_general(
-            inv_t[...], pair, NN, preferred_element_type=jnp.float32
-        ).astype(jnp.bfloat16)
+def finish(basis_in, ritz_in, basis_ref, ritz_ref, sem):
+    copies = [
+        pltpu.make_async_copy(basis_in, basis_ref, sem.at[0]),
+        pltpu.make_async_copy(ritz_in, ritz_ref, sem.at[1]),
+    ]
+    for copy in copies:
+        copy.start()
+    for copy in copies:
+        copy.wait()
 
 
 def shards(parts, stiffness_tiles, tile_cols, send_rows, block, lower_bound, upper_bound):
@@ -401,32 +431,33 @@
     dma = pltpu.SemaphoreType.DMA
     level = pltpu.VMEM((tiles + 2 * slots, modes, size), jnp.bfloat16)
     field = pltpu.VMEM((tiles, modes, size), jnp.bfloat16)
-    fields, inv_t, ritz = pl.pallas_call(
+    basis, ritz = pl.pallas_call(
         functools.partial(kernel, parts),
         out_shape=(
-            jax.ShapeDtypeStruct((2, tiles, modes, size), jnp.bfloat16),
-            jax.ShapeDtypeStruct((modes, width), jnp.bfloat16),
+            jax.ShapeDtypeStruct((modes, row_count), jnp.bfloat16),
             jax.ShapeDtypeStruct((width, width), jnp.float32),
         ),
         in_specs=[far] * 6,
-        out_specs=(hbm, vmem, vmem),
+        out_specs=(hbm, vmem),
         scratch_shapes=[
             pltpu.VMEM(stiffness_tiles.shape, jnp.bfloat16),
             pltpu.VMEM((tiles, nnz * size, size), jnp.bfloat16),
             level, level, level, pltpu.VMEM((modes, row_count), jnp.bfloat16), field, field, field,
             pltpu.VMEM((3, 2, slots, modes, size), jnp.bfloat16),
-            pltpu.VMEM((3, 8, 8, width), jnp.float32),
-            pltpu.VMEM((3 * parts, 8, width), jnp.float32),
-            pltpu.VMEM((3, 16, 8, width), jnp.float32),
-            pltpu.VMEM((3, 8, width), jnp.float32),
+            pltpu.VMEM((4, 8, 8, width), jnp.float32),
+            pltpu.VMEM((4 * parts, 8, width), jnp.float32),
+            pltpu.VMEM((4, 16, 8, width), jnp.float32),
+            pltpu.VMEM((4, 8, width), jnp.float32),
             pltpu.VMEM((modes, width), jnp.float32),
             pltpu.VMEM((modes, width), jnp.float32),
+            pltpu.VMEM((modes, width), jnp.bfloat16),
+            pltpu.VMEM((modes, row_count), jnp.bfloat16),
             pltpu.SMEM((nnz, tiles), jnp.int32),
             pltpu.SMEM(send_rows.shape, jnp.int32),
             pltpu.SMEM((1,), jnp.float32),
             pltpu.SMEM((1,), jnp.float32),
-            dma((5,)), dma((8,)), dma((2,)), dma((3, 2)), dma((3, 2)), dma((chunks,)), dma((chunks,)),
-            dma((3,)), dma((3,)), dma((3,)), dma((3,)),
+            dma((5,)), dma((8,)), dma((1,)), dma((3, 3)), dma((3, 3)), dma((chunks,)), dma((chunks,)),
+            dma((4,)), dma((4,)), dma((4,)), dma((4,)),
         ],
         compiler_params=pltpu.CompilerParams(
             collective_id=0, has_side_effects=True, vmem_limit_bytes=50331648
@@ -442,10 +473,11 @@
             jax.ShapeDtypeStruct((modes, row_count), jnp.bfloat16),
             jax.ShapeDtypeStruct((width, width), jnp.float32),
         ),
-        in_specs=[vmem, vmem, vmem],
-        out_specs=(vmem, vmem),
+        in_specs=[hbm, hbm],
+        out_specs=(hbm, hbm),
+        scratch_shapes=[dma((2,))],
         compiler_params=pltpu.CompilerParams(vmem_limit_bytes=8 * 1024 * 1024),
-    )(fields, inv_t, ritz)
+    )(basis, ritz)
     return basis.T, ritz
 
 

time: 42.3 us -> 41 us (0.969)
  Pallas kernels: 40.2 us -> 38.9 us
    pallas_call x1, Pallas kernels: 39.1 us -> 38.1 us  [shards(): pl.pallas_call(functools.partial(kernel, parts), out_shape=(jax.ShapeDtyp...]
where the time goes in v4:
time: 41 us; the launch traced here: 40.8 us
  Pallas kernels  38.9 us (95%)
  between operations  1.93 us (5%)
    pallas_call x1, Pallas kernels, shards(): pl.pallas_call(functools.partial(kernel, parts), out_shape=(jax.ShapeDtyp...  38.1 us
    pallas_call x1, Pallas kernels, shards(): pl.pallas_call(finish, out_shape=(jax.ShapeDtypeStruct((modes, row_count)...  0.82 us

profile of v4, /device:TPU:0, one launch (start us, length us, event | category | flops | bytes accessed | tf_op | source)
XLA Modules:
  0.0 40.8 jit_solution(4457179685016698940)
XLA Ops:
  1.9 38.1 %shard_map.77 = (bf16[64,4096]{1,0:T(8,128)(2,1)S(1)}, f32[128,128]{1,0:T(8,128)S(1)}) custom-call(s32[10,32]{1,0:T(8,128)} %bitcast.4, s32[2,8]{1,0:T(2,128)} %rows_hbm.1, f32[1]{0:T(128)S(6)} %copy.8.low_hbm, f32[1]{0:T(128)S(6)} %copy.9.high_hbm, bf16[64,4096]{1,0:T(8,128)(2,1)} %bitcast.3, bf16[32,10,128,128]{3,2,1,0:T(8,128)(2,1)} %a_hbm.1), custom_call_target="tpu_custom_call" | custom-call | tf_op jit(solution)/shard_map/pallas_call | solution.py:434
  40.0 0.8 %shard_map.78 = (bf16[64,4096]{1,0:T(8,128)(2,1)}, f32[128,128]{1,0:T(8,128)}) custom-call(bf16[64,4096]{1,0:T(8,128)(2,1)S(1)} %get-tuple-element.6.basis_in, f32[128,128]{1,0:T(8,128)S(1)} %get-tuple-element.7.ritz_in), custom_call_target="tpu_custom_call" | custom-call | tf_op jit(solution)/shard_map/pallas_call | solution.py:470

commit v5 on v4

--- a/solution.py
+++ b/solution.py
@@ -19,13 +19,14 @@
     parts, cols_hbm, rows_hbm, low_hbm, high_hbm, x_hbm, a_hbm, basis_ref, ritz_ref,
     a_ref, turned, level0, level1, level2, x_ref, plain, image, other, sends,
     shares, gathered, totals, sums, work, inv_ref, inv_t, basis,
-    cols, rows, low_ref, high_ref, x_sem, a_sem, keep_sem, halo_send, halo_recv, mode_send, mode_recv,
+    cols, rows, low_ref, high_ref, spread_sem, x_sem, a_sem, keep_sem, halo_send, halo_recv, mode_send, mode_recv,
     share_send, share_recv, total_send, total_recv,
 ):
     tiles, nnz, size = a_ref.shape[0], a_ref.shape[1], a_ref.shape[2]
     modes = x_hbm.shape[0]
     width = 2 * modes
     slots = rows.shape[1]
+    steps = parts.bit_length() - 1
     tables = [(cols_hbm, cols), (rows_hbm, rows), (low_hbm, low_ref), (high_hbm, high_ref)]
     tables = [pltpu.make_async_copy(*pair, x_sem.at[1 + i]) for i, pair in enumerate(tables)]
     chunks = mode_send.shape[0]
@@ -62,11 +63,27 @@
         ((d, e) for d in range(parts) for e in range(2) if d or e),
         key=lambda pair: (min(pair[0], parts - pair[0]), pair[1]),
     )
+    def flipped(bit):
+        return p + bit * (1 - 2 * ((p // bit) % 2))
+
+    partners = [(flipped(1 << b), my) for b in range(steps)] + [(p, 1 - my)]
     barrier = pltpu.get_barrier_semaphore()
-    for shift, other_mode in near_first:
-        pl.semaphore_signal(
-            barrier, inc=1, device_id=peer(shift, other_mode), device_id_type=MESH
-        )
+
+    @pl.when(has_far)
+    def _():
+        pl.semaphore_signal(barrier, inc=1, device_id=(far_slot, my), device_id_type=MESH)
+
+    for partner in partners:
+        pl.semaphore_signal(barrier, inc=1, device_id=partner, device_id_type=MESH)
+
+    def spread(stage):
+        if stage > 0:
+            pl.semaphore_wait(spread_sem.at[stage - 1], 1)
+        if stage < len(partners):
+            pl.semaphore_signal(
+                spread_sem.at[stage], inc=1, device_id=partners[stage], device_id_type=MESH
+            )
+
     fetch.wait()
     for load in loads[2:]:
         load.start()
@@ -89,7 +106,8 @@
         for level in (level0, level1, level2):
             level[tiles + slots :] = jnp.zeros((slots, modes, size), jnp.bfloat16)
 
-    pl.semaphore_wait(barrier, 2 * parts - 1)
+    pl.semaphore_wait(barrier, len(partners) + has_far.astype(jnp.int32))
+    spread(0)
 
     def halo(index, level, which):
         hop = 1 - odd if which == 2 else odd
@@ -173,9 +191,12 @@
                 for k in range(nnz):
                     turned[t, k * size : (k + 1) * size] = a_ref[t, k].T
 
+    spread(1)
     wait_halo(0, level0)
     send_tiles(1, level1, first)
+    spread(2)
     all_tiles(first, level1, 0, tiles)
+    spread(3)
     wait_halo(1, level1)
     half = tiles // 2
     quarter = half // 4
@@ -301,9 +322,12 @@
 
     for c in urgent:
         exchanged(c)
+    spread(4)
     send_tiles(2, level2, second)
     for c in later:
         exchanged(c)
+    for stage in range(5, len(partners) + 1):
+        spread(stage)
     share(0, fold(contract(level2, level2, 0, tiles)))
     wait_halo(2, level2)
     all_tiles(lambda t: product(level2, t).astype(jnp.bfloat16), image, 0, tiles)
@@ -317,7 +341,6 @@
     pair = jnp.concatenate([own_projected, mixed], axis=1)
     share(2, jnp.where(my == 0, pair, pltpu.roll(pair, modes, 1)))
     total(1)
-    total(2)
     rest_begin = my * half
     exchange(3, 1 - my).wait_recv()
     mixed = contract(image, other, rest_begin, half // 2)
@@ -365,6 +388,7 @@
 
         return inv_ref[...][:, modes:]
 
+    total(2)
     gram0, gram1 = arrived(0)
     gram0, gram1 = unfold(gram0), unfold(gram1)
     inv00 = factor_inverse(gram0)
@@ -423,7 +447,7 @@
     tiles, nnz, size = stiffness_tiles.shape[:3]
     slots = send_rows.shape[1]
     width = 2 * modes
-    assert parts >= 16 and parts % 2 == 0
+    assert parts >= 16 and parts & (parts - 1) == 0
     chunks = 5
     vmem = pl.BlockSpec(memory_space=pltpu.VMEM)
     hbm = pl.BlockSpec(memory_space=pl.ANY)
@@ -456,6 +480,7 @@
             pltpu.SMEM(send_rows.shape, jnp.int32),
             pltpu.SMEM((1,), jnp.float32),
             pltpu.SMEM((1,), jnp.float32),
+            pltpu.SemaphoreType.REGULAR((parts.bit_length(),)),
             dma((5,)), dma((8,)), dma((1,)), dma((3, 3)), dma((3, 3)), dma((chunks,)), dma((chunks,)),
             dma((4,)), dma((4,)), dma((4,)), dma((4,)),
         ],

time: 41 us -> 39 us (0.951)
  Pallas kernels: 38.9 us -> 36.9 us
    pallas_call x1, Pallas kernels: 38.1 us -> 36.1 us  [shards(): pl.pallas_call(functools.partial(kernel, parts), out_shape=(jax.ShapeDtyp...]
where the time goes in v5:
time: 39 us; the launch traced here: 38.8 us
  Pallas kernels  36.9 us (95%)
  between operations  1.93 us (5%)
    pallas_call x1, Pallas kernels, shards(): pl.pallas_call(functools.partial(kernel, parts), out_shape=(jax.ShapeDtyp...  36.1 us
    pallas_call x1, Pallas kernels, shards(): pl.pallas_call(finish, out_shape=(jax.ShapeDtypeStruct((modes, row_count)...  0.82 us

profile of v5, /device:TPU:0, one launch (start us, length us, event | category | flops | bytes accessed | tf_op | source)
XLA Modules:
  0.0 38.8 jit_solution(1816511841066465657)
XLA Ops:
  1.9 36.1 %shard_map.77 = (bf16[64,4096]{1,0:T(8,128)(2,1)S(1)}, f32[128,128]{1,0:T(8,128)S(1)}) custom-call(s32[10,32]{1,0:T(8,128)} %bitcast.4, s32[2,8]{1,0:T(2,128)} %rows_hbm.1, f32[1]{0:T(128)S(6)} %copy.8.low_hbm, f32[1]{0:T(128)S(6)} %copy.9.high_hbm, bf16[64,4096]{1,0:T(8,128)(2,1)} %bitcast.3, bf16[32,10,128,128]{3,2,1,0:T(8,128)(2,1)} %a_hbm.1), custom_call_target="tpu_custom_call" | custom-call | tf_op jit(solution)/shard_map/pallas_call | solution.py:458
  38.0 0.8 %shard_map.78 = (bf16[64,4096]{1,0:T(8,128)(2,1)}, f32[128,128]{1,0:T(8,128)}) custom-call(bf16[64,4096]{1,0:T(8,128)(2,1)S(1)} %get-tuple-element.6.basis_in, f32[128,128]{1,0:T(8,128)S(1)} %get-tuple-element.7.ritz_in), custom_call_target="tpu_custom_call" | custom-call | tf_op jit(solution)/shard_map/pallas_call | solution.py:495

commit v6 on v5

--- a/solution.py
+++ b/solution.py
@@ -27,6 +27,7 @@
     width = 2 * modes
     slots = rows.shape[1]
     steps = parts.bit_length() - 1
+    pieces_far = halo_send.shape[1] - 1
     tables = [(cols_hbm, cols), (rows_hbm, rows), (low_hbm, low_ref), (high_hbm, high_ref)]
     tables = [pltpu.make_async_copy(*pair, x_sem.at[1 + i]) for i, pair in enumerate(tables)]
     chunks = mode_send.shape[0]
@@ -110,15 +111,16 @@
     spread(0)
 
     def halo(index, level, which):
-        hop = 1 - odd if which == 2 else odd
-        count = slots if which == 2 else slots // 2
-        first_slot = slots // 2 if which == 1 else 0
+        near = which == pieces_far
+        hop = 1 - odd if near else odd
+        count = slots if near else slots // pieces_far
+        first_slot = 0 if near else which * count
         return pltpu.make_async_remote_copy(
-            src_ref=sends.at[index, which // 2, pl.ds(first_slot, count)],
+            src_ref=sends.at[index, int(near), pl.ds(first_slot, count)],
             dst_ref=level.at[pl.ds(tiles + slots * (1 - hop) + first_slot, count)],
             send_sem=halo_send.at[index, which],
             recv_sem=halo_recv.at[index, which],
-            device_id=(mate if which == 2 else far_slot, my),
+            device_id=(mate if near else far_slot, my),
             device_id_type=MESH,
         )
 
@@ -126,19 +128,19 @@
         pl.when(has_far)(halo(index, level, which).start)
 
     def start_near(index, level):
-        halo(index, level, 2).start()
+        halo(index, level, pieces_far).start()
 
     def wait_halo(index, level):
-        near = halo(index, level, 2)
+        near = halo(index, level, pieces_far)
         near.wait_recv()
         near.wait_send()
-        for which in range(2):
+        for which in range(pieces_far):
             copy = halo(index, level, which)
             pl.when(has_far)(copy.wait_recv)
             pl.when(has_far)(copy.wait_send)
 
-    start_far(0, level0, 0)
-    start_far(0, level0, 1)
+    for which in range(pieces_far):
+        start_far(0, level0, which)
     start_near(0, level0)
     for t in range(tiles):
         level0[t] = plain[t]
@@ -161,11 +163,11 @@
         return (2.0 * (product(level1, t) - center * own) * scale - before).astype(jnp.bfloat16)
 
     def send_tiles(index, level, make):
-        for which in range(2):
-            begin = which * (slots // 2)
-            made = [make(rows[odd, begin + u]) for u in range(slots // 2)]
+        count = slots // pieces_far
+        for which in range(pieces_far):
+            made = [make(rows[odd, which * count + u]) for u in range(count)]
             for u, value in enumerate(made):
-                sends[index, 0, begin + u] = value
+                sends[index, 0, which * count + u] = value
             start_far(index, level, which)
         made = [make(rows[1 - odd, u]) for u in range(slots)]
         for u, value in enumerate(made):
@@ -228,12 +230,12 @@
     base = (parts - 8) // 2
 
     def owners(k):
-        return [base + b for b in range(8)] if k == 2 else [base + k % 2 + 2 * b for b in range(4)]
+        return [base + k % 2 + 2 * b for b in range(4)]
 
     def owned(k):
         place = p - base
         inside = (place >= 0) & (place < 8)
-        return inside if k == 2 else inside & (lax.rem(p - base + parts, 2) == k % 2)
+        return inside & (lax.rem(place + parts, 2) == k % 2)
 
     def blocks_wait(ref, count, sem):
         view = ref.at[pl.ds(0, count)]
@@ -331,19 +333,17 @@
     share(0, fold(contract(level2, level2, 0, tiles)))
     wait_halo(2, level2)
     all_tiles(lambda t: product(level2, t).astype(jnp.bfloat16), image, 0, tiles)
+    share(2, fold(contract(image, level2, 0, tiles)))
     for c in urgent:
         exchange(c, 1 - my).wait_recv()
     cross = contract(level2, other, (1 - my) * half, half)
     share(1, fold(jnp.where(my == 0, cross, cross.T)))
+    mixed = contract(image, other, (1 - my) * half, half)
     total(0)
-    own_projected = contract(image, level2, 0, tiles)
-    mixed = contract(image, other, (1 - my) * half, half)
-    pair = jnp.concatenate([own_projected, mixed], axis=1)
-    share(2, jnp.where(my == 0, pair, pltpu.roll(pair, modes, 1)))
     total(1)
     rest_begin = my * half
     exchange(3, 1 - my).wait_recv()
-    mixed = contract(image, other, rest_begin, half // 2)
+    mixed = mixed + contract(image, other, rest_begin, half // 2)
     exchange(4, 1 - my).wait_recv()
     share(3, fold(mixed + contract(image, other, rest_begin + half // 2, half // 2)))
 
@@ -414,12 +414,12 @@
         ).astype(jnp.bfloat16)
     keep = pltpu.make_async_copy(basis, basis_ref, keep_sem.at[0])
     keep.start()
-    projected_t = jnp.concatenate(arrived(2), axis=0)
+    own0, own1 = arrived(2)
     late0, late1 = arrived(3)
-    projected_t = projected_t + jnp.concatenate(
+    projected_t = jnp.concatenate(
         [
-            jnp.concatenate([blank, unfold(late0)], axis=1),
-            jnp.concatenate([unfold(late1), blank], axis=1),
+            jnp.concatenate([unfold(own0), unfold(late0)], axis=1),
+            jnp.concatenate([unfold(late1), unfold(own1)], axis=1),
         ],
         axis=0,
     )
@@ -468,9 +468,9 @@
             pltpu.VMEM((tiles, nnz * size, size), jnp.bfloat16),
             level, level, level, pltpu.VMEM((modes, row_count), jnp.bfloat16), field, field, field,
             pltpu.VMEM((3, 2, slots, modes, size), jnp.bfloat16),
+            pltpu.VMEM((4, 4, 8, width), jnp.float32),
+            pltpu.VMEM((4 * parts, 8, width), jnp.float32),
             pltpu.VMEM((4, 8, 8, width), jnp.float32),
-            pltpu.VMEM((4 * parts, 8, width), jnp.float32),
-            pltpu.VMEM((4, 16, 8, width), jnp.float32),
             pltpu.VMEM((4, 8, width), jnp.float32),
             pltpu.VMEM((modes, width), jnp.float32),
             pltpu.VMEM((modes, width), jnp.float32),

time: 39 us -> 38.9 us (level)
  no operation moved by 1% of the time
where the time goes in v6:
time: 38.9 us; the launch traced here: 38.7 us
  Pallas kernels  36.8 us (95%)
  between operations  1.93 us (5%)
    pallas_call x1, Pallas kernels, shards(): pl.pallas_call(functools.partial(kernel, parts), out_shape=(jax.ShapeDtyp...  36 us
    pallas_call x1, Pallas kernels, shards(): pl.pallas_call(finish, out_shape=(jax.ShapeDtypeStruct((modes, row_count)...  0.82 us

profile of v6, /device:TPU:0, one launch (start us, length us, event | category | flops | bytes accessed | tf_op | source)
XLA Modules:
  0.0 38.7 jit_solution(3792505447947026255)
XLA Ops:
  1.9 36.0 %shard_map.77 = (bf16[64,4096]{1,0:T(8,128)(2,1)S(1)}, f32[128,128]{1,0:T(8,128)S(1)}) custom-call(s32[10,32]{1,0:T(8,128)} %bitcast.4, s32[2,8]{1,0:T(2,128)} %rows_hbm.1, f32[1]{0:T(128)S(6)} %copy.8.low_hbm, f32[1]{0:T(128)S(6)} %copy.9.high_hbm, bf16[64,4096]{1,0:T(8,128)(2,1)} %bitcast.3, bf16[32,10,128,128]{3,2,1,0:T(8,128)(2,1)} %a_hbm.1), custom_call_target="tpu_custom_call" | custom-call | tf_op jit(solution)/shard_map/pallas_call | solution.py:458
  37.9 0.8 %shard_map.78 = (bf16[64,4096]{1,0:T(8,128)(2,1)}, f32[128,128]{1,0:T(8,128)}) custom-call(bf16[64,4096]{1,0:T(8,128)(2,1)S(1)} %get-tuple-element.6.basis_in, f32[128,128]{1,0:T(8,128)S(1)} %get-tuple-element.7.ritz_in), custom_call_target="tpu_custom_call" | custom-call | tf_op jit(solution)/shard_map/pallas_call | solution.py:495

commit v7 on v6

--- a/solution.py
+++ b/solution.py
@@ -203,9 +203,11 @@
     half = tiles // 2
     quarter = half // 4
     pieces = [(0, quarter), (quarter, quarter), (2 * quarter, 2 * quarter)]
-    pieces = [(0, *piece) for piece in pieces] + [(1, 0, half // 2), (1, half // 2, half // 2)]
+    pieces = [(0, *piece) for piece in pieces] + [
+        (1, 0, half // 2), (1, half // 2, quarter), (1, half // 2 + quarter, quarter)
+    ]
     urgent = range(3)
-    later = range(3, 5)
+    later = range(3, 6)
 
     def exchange(c, sender):
         which, offset, count = pieces[c]
@@ -344,7 +346,8 @@
     rest_begin = my * half
     exchange(3, 1 - my).wait_recv()
     mixed = mixed + contract(image, other, rest_begin, half // 2)
-    exchange(4, 1 - my).wait_recv()
+    for c in (4, 5):
+        exchange(c, 1 - my).wait_recv()
     share(3, fold(mixed + contract(image, other, rest_begin + half // 2, half // 2)))
 
     step = 16
@@ -448,7 +451,7 @@
     slots = send_rows.shape[1]
     width = 2 * modes
     assert parts >= 16 and parts & (parts - 1) == 0
-    chunks = 5
+    chunks = 6
     vmem = pl.BlockSpec(memory_space=pltpu.VMEM)
     hbm = pl.BlockSpec(memory_space=pl.ANY)
     far = pl.BlockSpec(memory_space=pltpu.HBM)

time: 38.9 us -> 38.9 us (level)
  no operation moved by 1% of the time
where the time goes in v7:
time: 38.9 us; the launch traced here: 38.7 us
  Pallas kernels  36.8 us (95%)
  between operations  1.93 us (5%)
    pallas_call x1, Pallas kernels, shards(): pl.pallas_call(functools.partial(kernel, parts), out_shape=(jax.ShapeDtyp...  36 us
    pallas_call x1, Pallas kernels, shards(): pl.pallas_call(finish, out_shape=(jax.ShapeDtypeStruct((modes, row_count)...  0.82 us

profile of v7, /device:TPU:0, one launch (start us, length us, event | category | flops | bytes accessed | tf_op | source)
XLA Modules:
  0.0 38.7 jit_solution(12384780326622943589)
XLA Ops:
  1.9 36.0 %shard_map.77 = (bf16[64,4096]{1,0:T(8,128)(2,1)S(1)}, f32[128,128]{1,0:T(8,128)S(1)}) custom-call(s32[10,32]{1,0:T(8,128)} %bitcast.4, s32[2,8]{1,0:T(2,128)} %rows_hbm.1, f32[1]{0:T(128)S(6)} %copy.8.low_hbm, f32[1]{0:T(128)S(6)} %copy.9.high_hbm, bf16[64,4096]{1,0:T(8,128)(2,1)} %bitcast.3, bf16[32,10,128,128]{3,2,1,0:T(8,128)(2,1)} %a_hbm.1), custom_call_target="tpu_custom_call" | custom-call | tf_op jit(solution)/shard_map/pallas_call | solution.py:461
  37.9 0.8 %shard_map.78 = (bf16[64,4096]{1,0:T(8,128)(2,1)}, f32[128,128]{1,0:T(8,128)}) custom-call(bf16[64,4096]{1,0:T(8,128)(2,1)S(1)} %get-tuple-element.6.basis_in, f32[128,128]{1,0:T(8,128)S(1)} %get-tuple-element.7.ritz_in), custom_call_target="tpu_custom_call" | custom-call | tf_op jit(solution)/shard_map/pallas_call | solution.py:498
